TPU v7x, 32 devices: a 4x2x2 block of a 4x4x8 slice. The times are simulated.
32 devices in a mesh: mp: 4 (over y, z), fsdp: 8 (over x, core).
Axes of the slice: x: 4, y: 2, z: 2, core: 2. Of those that a mesh axis runs over, the one named last changes fastest.
The devices are a block of a 4x4x8 slice.
Arguments:
- x: bfloat16 [2, 32, 2048, 768], P(None, ('mp', 'fsdp')), parts along dimension 1
- dy: bfloat16 [32, 2048, 768], P(('mp', 'fsdp')), parts along dimension 0
- xn: bfloat16 [32, 2048, 768], P(('mp', 'fsdp')), parts along dimension 0
- w1: float32 [2, 3072, 3072], P(None, ('mp', 'fsdp')), parts along dimension 1
- w2: float32 [2, 12288, 768], P(None, ('mp', 'fsdp')), parts along dimension 1
- g1: float32 [2, 3072, 3072], P(None, ('mp', 'fsdp')), parts along dimension 1
- g2: float32 [2, 12288, 768], P(None, ('mp', 'fsdp')), parts along dimension 1
- m1: float32 [2, 3072, 3072], P(None, ('mp', 'fsdp')), parts along dimension 1
- m2: float32 [2, 12288, 768], P(None, ('mp', 'fsdp')), parts along dimension 1
- v1: float32 [2, 3072, 3072], P(None, ('mp', 'fsdp')), parts along dimension 1
- v2: float32 [2, 12288, 768], P(None, ('mp', 'fsdp')), parts along dimension 1
- hp: float32 [5], replicated
- step: int32 [1], replicated
Outputs:
- output 1: float32 [2, 3072, 3072], P(None, ('mp', 'fsdp')), parts along dimension 1
- output 2: float32 [2, 12288, 768], P(None, ('mp', 'fsdp')), parts along dimension 1
- output 3: float32 [2, 3072, 3072], P(None, ('mp', 'fsdp')), parts along dimension 1
- output 4: float32 [2, 12288, 768], P(None, ('mp', 'fsdp')), parts along dimension 1
- output 5: float32 [2, 3072, 3072], P(None, ('mp', 'fsdp')), parts along dimension 1
- output 6: float32 [2, 12288, 768], P(None, ('mp', 'fsdp')), parts along dimension 1
- output 7: bfloat16 [32, 2048, 768], P(('mp', 'fsdp')), parts along dimension 0
There are 4 independent parts. A program takes and returns all parts, laid end to end along the dimension named above; an argument that names none is the same for every part.
All inputs are finite; a program needn't handle non-finite values.
Results may differ from a plain program's by a relative error of at most 0.00683772.
Values are sent between devices in bfloat16 or wider.
A program may use at most 768 MiB of HBM per device.

v0:
```python
import functools

import jax
import jax.numpy as jnp
from jax import lax
from jax.experimental import pallas as pl
from jax.experimental.pallas import tpu as pltpu
from jax.sharding import PartitionSpec as P

F32 = jnp.float32
BF = jnp.bfloat16
TM = 512
TF = 1024
GC = 0.7978845608028654
GA = 0.044715


def gelu(h):
    return h * (0.5 * (1.0 + jnp.tanh(GC * (h + GA * (h * h * h)))))


def gelu_grad(h):
    s = h * h
    t = jnp.tanh(GC * (h + GA * (s * h)))
    cdf = 0.5 + 0.5 * t
    dt = (0.5 * GC) * (1.0 - t * t) * (1.0 + (3.0 * GA) * s)
    return h * cdf, cdf + h * dt


def dot(a, b):
    return jnp.dot(a, b, preferred_element_type=F32)


def dot_t(a, b):
    return lax.dot_general(a, b, (((1,), (1,)), ((), ())), preferred_element_type=F32)


def offset(j):
    if isinstance(j, int):
        return (2, 1, 3, 0)[j]
    return jnp.where(j == 0, 2, jnp.where(j == 1, 1, jnp.where(j == 2, 3, 0)))


def ipow(b, t):
    r = b * b
    for e in (3, 4, 5):
        r = r * jnp.where(t >= e, b, 1.0)
    return r


def kernel(n, x, dy, xn, w1, w2, g1, g2, m1, m2, v1, v2, hp, step,
           w1n, w2n, m1n, m2n, v1n, v2n, zo, go, gn, rp,
           xb, xt, yb, yt, ab, db, acc, p1, p2, pq, tb, ra, rb, nb, w1s, w2s,
           ag_s, ag_r, rs_s, rs_r, wsem, lsem, osem):
    nl, T, D = x.shape
    R = w2.shape[1]
    FB = 2 * R
    H = R // 2
    nc = n // 2
    D8 = D // n
    nt = T // TM
    me = lax.axis_index('fsdp')
    c = lax.div(me, 2)
    k = lax.rem(me, 2)
    cl, cr, co = lax.rem(c + nc - 1, nc), lax.rem(c + 1, nc), lax.rem(c + 2, nc)
    i, iq = 2 * c + k, 2 * c + 1 - k
    il, ir, io = 2 * cl + k, 2 * cr + k, 2 * co + k
    ilq, irq, ioq = 2 * cl + 1 - k, 2 * cr + 1 - k, 2 * co + 1 - k
    hA, hB = pl.ds(0, H), pl.ds(H, H)
    LEFT, RIGHT, MATE = il, ir, iq

    barrier = pltpu.get_barrier_semaphore()
    for dev in (LEFT, RIGHT, MATE):
        pl.semaphore_signal(barrier, inc=1, device_id={'fsdp': dev})

    pending = {}

    def rmake(src, dst, ss, rs, dev):
        return pltpu.make_async_remote_copy(
            src_ref=src[0].at[src[1:]], dst_ref=dst[0].at[dst[1:]], send_sem=ss[0].at[ss[1:]],
            recv_sem=rs[0].at[rs[1:]], device_id={'fsdp': dev})

    def rcopy(key, *a):
        rmake(*a).start()
        pending[key] = a

    def rwait(dst, ss, rs, dev):
        rmake(dst, dst, ss, rs, dev).wait_recv()

    def sent(key):
        a = pending.pop(key, None)
        if a is not None:
            rmake(*a).wait_send()

    class Gather:
        def __init__(self, ph, m, G, src):
            self.a, self.m, self.G, self.src = ph * 4 + m, m, G, src

        def put(self, t, src, dst, dev):
            rcopy(('ag', self.a, t), src, dst, (ag_s, self.a, t), (ag_r, self.a, t), dev)

        def got(self, t, dst, dev):
            rwait(dst, (ag_s, self.a, t), (ag_r, self.a, t), dev)

        def start(self):
            self.start_a()
            self.start_b()

        def fwd(self):
            self.fwd_a()
            self.fwd_b()

        def start_a(self):
            G, m, src = self.G, self.m, self.src
            self.put(0, src + (hA,), (G, m, i, hA), RIGHT)
            self.put(3, src + (hB,), (G, m, i, hB), LEFT)
            self.put(4, src, (G, m, i), MATE)

        def start_b(self):
            G, m, src = self.G, self.m, self.src
            self.put(1, src + (hB,), (G, m, i, hB), RIGHT)
            self.put(2, src + (hA,), (G, m, i, hA), LEFT)

        def fwd_a(self):
            G, m = self.G, self.m
            self.got(0, (G, m, il, hA), LEFT)
            self.put(5, (G, m, il, hA), (G, m, il, hA), RIGHT)
            self.got(3, (G, m, ir, hB), RIGHT)
            self.put(6, (G, m, ir, hB), (G, m, ir, hB), LEFT)

        def fwd_b(self):
            G, m = self.G, self.m
            self.got(1, (G, m, il, hB), LEFT)
            self.put(7, (G, m, il), (G, m, il), MATE)
            self.got(2, (G, m, ir, hA), RIGHT)
            self.put(8, (G, m, ir), (G, m, ir), MATE)

        def fin(self):
            G, m = self.G, self.m
            self.got(5, (G, m, io, hA), LEFT)
            self.got(6, (G, m, io, hB), RIGHT)
            self.put(9, (G, m, io), (G, m, io), MATE)

        def mate(self, t):
            G, m = self.G, self.m
            j = {4: iq, 7: ilq, 8: irq, 9: ioq}[t]
            self.got(t, (G, m, j), MATE)

        def full(self):
            for t in (4, 7, 8, 9):
                self.mate(t)

    old = [Gather(0, m, go, (nb, m)) for m in range(2 * nl)]
    new = [Gather(1, m, gn, (nb, m)) for m in range(2 * nl)]

    dest = (co, cr, cl, c)
    mine = tuple(2 * d + k for d in dest)
    theirs = tuple(2 * d + 1 - k for d in dest)

    def rset(m):
        return 1 - m % 2

    def part(m):
        return p2 if m % 2 else p1

    def rput(m, t, src, dst, dev):
        rcopy(('rs', m, t), src, dst, (rs_s, m, t), (rs_r, m, t), dev)

    def rgot(m, t, dst, dev):
        rwait(dst, (rs_s, m, t), (rs_r, m, t), dev)

    def x0_copy(m, sl):
        return rmake((part(m), theirs[sl]), (pq, rset(m), sl), (rs_s, m, sl), (rs_r, m, sl), MATE)

    def rs_x0(m, sl):
        x0_copy(m, sl).start()

    def rs_pair(m, sl):
        s = rset(m)
        for t in {0: (4, 5), 1: (6,), 2: (7,), 3: ()}[sl]:
            sent(('rs', m + 2, t))
        rgot(m, sl, (pq, s, sl), MATE)
        x0_copy(m, sl).wait_send()
        tb[s, sl] = part(m)[mine[sl]].astype(F32) + pq[s, sl].astype(F32)
        if sl == 0:
            rput(m, 4, (tb, s, 0, hA), (ra, m), LEFT)
            rput(m, 5, (tb, s, 0, hB), (rb, m), RIGHT)
        elif sl == 1:
            rput(m, 6, (tb, s, 1, hA), (rp, m, 0, hA), RIGHT)
        elif sl == 2:
            rput(m, 7, (tb, s, 2, hB), (rp, m, 1, hB), LEFT)

    def rs_mid(m):
        s = rset(m)
        rgot(m, 4, (ra, m), RIGHT)
        ra[m] = ra[m] + tb[s, 2, hA]
        rput(m, 8, (ra, m), (rp, m, 1, hA), LEFT)
        rgot(m, 5, (rb, m), LEFT)
        rb[m] = rb[m] + tb[s, 1, hB]
        rput(m, 9, (rb, m), (rp, m, 0, hB), RIGHT)

    def pieces(m, arr, row):
        l = m // 2
        if m % 2:
            return [(arr.at[l], acc.at[pl.ds(row, R)])]
        return [(arr.at[l, :, pl.ds(q * FB, FB)], acc.at[pl.ds(row + q * D8, D8)]) for q in range(nc)]

    ins = {0: (w1, g1, m1, v1), 1: (w2, g2, m2, v2)}
    outs = {0: (w1n, m1n, v1n), 1: (w2n, m2n, v2n)}

    def adam_copies(m):
        cps = []
        for j, arr in enumerate(ins[m % 2]):
            for hbm, vm in pieces(m, arr, j * R):
                cps.append(pltpu.make_async_copy(hbm, vm, lsem.at[len(cps)]))
        return cps

    def adam_load(m):
        for cp in adam_copies(m):
            cp.start()

    def adam_outs(m):
        cps = []
        for arr, row in zip(outs[m % 2], (0, 2 * R, 3 * R)):
            for hbm, vm in pieces(m, arr, row):
                cps.append(pltpu.make_async_copy(vm, hbm, osem.at[len(cps)]))
        return cps

    def adam_run(m):
        s = rset(m)
        for t, dst, dev in ((6, (rp, m, 0, hA), LEFT), (9, (rp, m, 0, hB), LEFT),
                            (8, (rp, m, 1, hA), RIGHT), (7, (rp, m, 1, hB), RIGHT)):
            rgot(m, t, dst, dev)
        cps = [pltpu.make_async_copy(rp.at[m, e], acc.at[pl.ds((4 + e) * R, R)], lsem.at[16 + e])
               for e in range(2)]
        for cp in cps:
            cp.start()
        for cp in adam_copies(m) + cps:
            cp.wait()
        for t in range(5):
            sent(('ag', m, t))
        lr, b1, b2, eps, wd = [hp[j] for j in range(5)]
        c1 = 1.0 - ipow(b1, step[0])
        c2 = 1.0 - ipow(b2, step[0])
        ch = 32

        @pl.loop(0, R // ch)
        def _(e):
            o = pl.multiple_of(e * ch, ch)
            rows = [pl.ds(j * R + o, ch) for j in range(6)]
            S = tb[s, 3, pl.ds(o, ch)] + acc[rows[4]] + acc[rows[5]]
            w = acc[rows[0]]
            g = (acc[rows[1]] + S) * 0.5
            mn = b1 * acc[rows[2]] + (1.0 - b1) * g
            vn = b2 * acc[rows[3]] + (1.0 - b2) * g * g
            upd = (mn / c1) / (jnp.sqrt(vn / c2) + eps)
            wn = w - lr * (upd + wd * w)
            acc[rows[0]] = wn
            acc[rows[2]] = mn
            acc[rows[3]] = vn
            nb[m, pl.ds(o, ch)] = wn.astype(BF)

        for cp in adam_outs(m):
            cp.start()

    def adam_done(m):
        for cp in adam_outs(m):
            cp.wait()

    def wcopy(G, l, q, slot, kind):
        if kind:
            return pltpu.make_async_copy(G.at[2 * l + 1, pl.ds(2 * q, 2)], w2s.at[slot], wsem.at[slot, 1])
        return pltpu.make_async_copy(G.at[2 * l, :, pl.ds(q * D8, D8)], w1s.at[slot], wsem.at[slot, 0])

    def wcopies(*a):
        return wcopy(*a, 0), wcopy(*a, 1)

    def wload(*a):
        for cp in wcopies(*a):
            cp.start()

    def wwait(*a):
        for cp in wcopies(*a):
            cp.wait()

    def tile(t):
        return pl.ds(pl.multiple_of(t * TM, TM), TM)

    def w1v(slot):
        return w1s[slot].reshape(D, FB)

    def w2v(slot):
        return w2s[slot].reshape(FB, D)

    def bwd_fused(slot):
        @pl.loop(0, nt)
        def _(t):
            r = tile(t)
            h = dot(xb[r, :], w1v(slot))
            da = dot_t(yb[r, :], w2v(slot))
            a, gp = gelu_grad(h)
            ab[r, :] = a.astype(BF)
            db[r, :] = (da * gp).astype(BF)

    def bwd_p2(q):
        @pl.loop(0, D // 256)
        def _(t):
            o = pl.ds(pl.multiple_of(t * 256, 256), 256)
            r = dot(yt[o, :], ab[...])
            p2[pl.ds(2 * q, 2), :, o] = r.T.astype(BF).reshape(2, R, 256)

    def bwd_p1(q):
        @pl.loop(0, 2)
        def _(t):
            o = pl.ds(pl.multiple_of(t * (D // 2), D // 2), D // 2)
            r = dot(xt[o, :], db[...])
            p1[pl.ds(t * (n // 2), n // 2), pl.ds(pl.multiple_of(q * D8, D8), D8), :] = (
                r.astype(BF).reshape(n // 2, D8, FB))

    def bwd_dx(slot, first):
        @pl.loop(0, nt)
        def _(t):
            r = tile(t)
            z = dot_t(db[r, :], w1v(slot))
            acc[r, :] = jnp.where(first, yb[r, :].astype(F32), acc[r, :]) + z

    def transpose(dst, src):
        @pl.loop(0, T // 256)
        def _(t):
            o = pl.ds(pl.multiple_of(t * 256, 256), 256)
            dst[:, o] = src[o, :].T

    order = (c, cr, cl, co)
    abuf = (ab, db, yb, xb)

    def hidden(l, hooks):
        cps = [wcopy(gn, l, order[j], j % 2, 0) for j in range(nc)]
        cps[0].start()
        for j in range(nc):
            if j + 1 < nc:
                cps[j + 1].start()
            cps[j].wait()

            @pl.loop(0, nt)
            def _(t):
                r = tile(t)
                xv = xb[r, :]
                if j == 0:
                    acc[r, :] = xv.astype(F32)
                abuf[j][r, :] = gelu(dot(xv, w1v(j % 2))).astype(BF)
            if j in hooks:
                with jax.named_scope(f'hookH{j}'):
                    hooks[j]()

    def project(l, ready, hooks, done, late):
        cps = [wcopy(gn, l, order[j], j % 2, 1) for j in range(nc)]
        ready(0)
        cps[0].start()
        for j in range(nc):
            if j + 1 < late:
                with jax.named_scope(f'ready{j + 1}'):
                    ready(j + 1)
                cps[j + 1].start()
            elif j >= late:
                with jax.named_scope(f'ready{j}'):
                    ready(j)
                cps[j].start()
            cps[j].wait()

            @pl.loop(0, nt)
            def _(t):
                r = tile(t)
                z = acc[r, :] + dot(abuf[j][r, :], w2v(j % 2))
                if j == nc - 1:
                    xb[r, :] = z.astype(BF)
                    done(t)
                else:
                    acc[r, :] = z
            if j in hooks:
                with jax.named_scope(f'hookP{j}'):
                    hooks[j]()

    def narrow(dst):
        @pl.loop(0, nt)
        def _(t):
            r = tile(t)
            dst[r, :] = acc[r, :].astype(BF)

    def at(j, hooks):
        for jj, fn in hooks.items():
            @pl.when(j == jj)
            def _():
                fn()

    def blocks(G, l, off, count, stages, ready=None):
        wload(G, l, lax.rem(c + off(0), nc), 0)

        @pl.loop(0, count)
        def _(j):
            s = lax.rem(j, 2)
            q = lax.rem(c + off(j), nc)

            @pl.when(j + 1 < count)
            def _():
                wload(G, l, lax.rem(c + off(j + 1), nc), 1 - s)
            wwait(G, l, q, s)
            for name, fn, hooks in stages:
                with jax.named_scope(name):
                    fn(j, q, s)
                with jax.named_scope(name + 'Hook'):
                    at(j, hooks)

    scope = jax.named_scope

    with scope('start'):
        w_in = [[pltpu.make_async_copy(a, b, lsem.at[m * 4 + e])
                 for e, (a, b) in enumerate(pieces(m, ins[m % 2][0], m * R))] for m in range(2 * nl)]
        for m in (2, 3, 0, 1):
            for cp in w_in[m]:
                cp.start()
        tok_in = [pltpu.make_async_copy(x.at[1], xb, wsem.at[0, 0]),
                  pltpu.make_async_copy(dy, yb, wsem.at[0, 1])]
        for cp in tok_in:
            cp.start()
        own_out = [pltpu.make_async_copy(nb.at[m], go.at[m, i], osem.at[m]) for m in range(2 * nl)]
        for m in (2, 3, 0, 1):
            for cp in w_in[m]:
                cp.wait()
            nb[m] = acc[pl.ds(m * R, R), :].astype(BF)
            if m == 2:
                pl.semaphore_wait(barrier, 3)
            if m >= 2:
                old[m].start()
            own_out[m].start()
        for cp in tok_in:
            cp.wait()
    with scope('f2'):
        old[2].fwd()
    with scope('xt'):
        transpose(xt, xb)
        for cp in own_out:
            cp.wait()
    with scope('f3'):
        old[3].fwd()
        old[0].start()
        old[1].start()
    with scope('yt'):
        transpose(yt, yb)
    with scope('full23'):
        old[2].fin()
        old[2].full()
        old[3].fin()
        old[3].full()

    def c2_2():
        old[0].fin()
        rs_pair(3, 2)

    def c2_3():
        old[1].fin()
        for sl in range(4):
            rs_x0(2, sl)
        rs_pair(3, 3)

    blocks(go, 1, offset, nc, [
        ('A2', lambda j, q, s: bwd_fused(s), {2: lambda: rs_pair(3, 1), 3: lambda: rs_mid(3)}),
        ('B2', lambda j, q, s: bwd_p2(q), {
            0: lambda: rs_x0(3, 0),
            1: lambda: (rs_x0(3, 1), rs_pair(3, 0)),
            2: lambda: rs_x0(3, 2),
            3: lambda: rs_x0(3, 3)}),
        ('C2', lambda j, q, s: bwd_p1(q), {
            0: old[0].fwd, 1: old[1].fwd, 2: c2_2, 3: c2_3}),
        ('D2', lambda j, q, s: bwd_dx(s, j == 0), {}),
    ])
    with scope('mid2'):
        xin = pltpu.make_async_copy(x.at[0], xb, lsem.at[0])
        xin.start()
        for sl in range(4):
            rs_pair(2, sl)
    with scope('tr2'):
        narrow(yb)
        transpose(yt, yb)
        xin.wait()
        transpose(xt, xb)
    with scope('full01'):
        old[0].full()
        old[1].full()

    adam_load(3)

    def up3():
        rs_pair(1, 0)
        adam_run(3)

    def up2():
        adam_done(3)
        adam_load(2)

    def up1():
        rs_pair(1, 2)
        adam_run(2)

    blocks(go, 0, offset, nc, [
        ('A1', lambda j, q, s: bwd_fused(s), {
            1: lambda: rs_mid(2), 2: lambda: rs_pair(1, 1), 3: up1}),
        ('B1', lambda j, q, s: bwd_p2(q), {jj: functools.partial(rs_x0, 1, jj) for jj in range(nc)}),
        ('C1', lambda j, q, s: bwd_p1(q), {1: up3, 2: up2}),
    ])
    with scope('mid1'):
        for sl in range(4):
            rs_x0(0, sl)
        xin = pltpu.make_async_copy(xn, xb, wsem.at[0, 0])
        xin.start()
        adam_done(2)
        adam_load(1)
        rs_mid(1)
        rs_pair(1, 3)
        for sl in range(4):
            rs_pair(0, sl)
    with scope('adam1'):
        adam_run(1)
        adam_done(1)
        adam_load(0)
    with scope('mid0'):
        rs_mid(0)
        new[1].start_a()
    own_out = [pltpu.make_async_copy(nb.at[m], gn.at[m, i], wsem.at[m // 2, m % 2]) for m in range(2 * nl)]
    with scope('adam0'):
        xin.wait()
        adam_run(0)
        new[0].start()
        for cp in own_out:
            cp.start()
    with scope('fn0'):
        new[0].fwd_a()
        new[1].start_b()
        new[1].fwd_a()
        new[0].fwd_b()
        for cp in own_out:
            cp.wait()
        adam_done(0)
    with scope('full_n0'):
        new[0].fin()
        new[2].start()
        new[0].full()

    def nx2():
        new[2].fwd_a()
        new[3].start()

    with scope('H1'):
        hidden(0, {1: new[1].fwd_b, 3: new[1].fin})
    with scope('P1'):
        project(0, lambda j: new[1].mate((4, 8, 7, 9)[j]), {0: nx2, 2: new[2].fwd_b}, lambda t: None, nc)
    with scope('full_n2'):
        new[2].fin()
        new[2].full()

    w1c = [wcopy(gn, 1, order[j], j % 2, 0) for j in range(nc)]
    w2c = [wcopy(gn, 1, order[j], j % 2, 1) for j in range(nc)]

    def step(hj=None, pj=None, last=False, hook=None):
        @pl.loop(0, T // TF)
        def _(t):
            r = pl.ds(pl.multiple_of(t * TF, TF), TF)
            if hook is not None:
                @pl.when(t == T // TF - 1)
                def _():
                    hook()
            if pj is not None:
                z = acc[r, :] + dot(abuf[pj][r, :], w2v(pj % 2))
            if hj is not None:
                xv = xb[r, :]
                if hj == 0:
                    acc[r, :] = xv.astype(F32)
                abuf[hj][r, :] = gelu(dot(xv, w1v(hj % 2))).astype(BF)
            if last:
                xb[r, :] = z.astype(BF)
                zout(t).start()
            elif pj is not None:
                acc[r, :] = z

    def zout(t):
        r = pl.ds(t * TF if isinstance(t, int) else pl.multiple_of(t * TF, TF), TF)
        return pltpu.make_async_copy(xb.at[r], zo.at[r], lsem.at[t])

    with scope('F2a'):
        new[3].mate(4)
        w1c[0].start()
        w2c[0].start()
        w1c[1].start()
        w1c[0].wait()
        step(hj=0)
    with scope('F2b'):
        new[3].fwd_a()
        w1c[2].start()
        w1c[1].wait()
        w2c[0].wait()
        step(hj=1, pj=0)
    def right_in():
        new[3].mate(8)
        new[3].mate(7)
        w2c[1].start()
        w2c[2].start()

    def opposite_in():
        new[3].mate(9)
        w2c[3].start()

    with scope('F2c'):
        new[3].fwd_b()
        w1c[3].start()
        w1c[2].wait()
        step(hj=2, hook=right_in)
    with scope('F2d'):
        w1c[3].wait()
        w2c[1].wait()
        step(hj=3, pj=1, hook=new[3].fin)
    with scope('F2e'):
        w2c[2].wait()
        step(pj=2, hook=opposite_in)
    with scope('F2f'):
        w2c[3].wait()
        step(pj=3, last=True)
    with scope('end'):
        for t in range(T // TF):
            zout(t).wait()
        for key in list(pending):
            sent(key)


def copy_out(*refs):
    m = (len(refs) - 2) // 3
    src, out, bufs, isem, osem = refs[:m], refs[m:2 * m], refs[2 * m:3 * m], refs[-2], refs[-1]
    ins, outs = [], []
    for e in range(m):
        h = src[e].shape[0] // 2
        for p in range(2):
            v = pl.ds(p * h, h)
            ins.append(pltpu.make_async_copy(src[e].at[v], bufs[e].at[v], isem.at[e, p]))
            outs.append(pltpu.make_async_copy(bufs[e].at[v], out[e].at[v], osem.at[e, p]))
    for cp in ins:
        cp.start()
    for a, b in zip(ins, outs):
        a.wait()
        b.start()
    for cp in outs:
        cp.wait()


def solution(mesh):
    n = mesh.shape['fsdp']
    tok4 = P(None, ('mp', 'fsdp'), None, None)
    tok3 = P(('mp', 'fsdp'), None, None)
    rows = P(None, ('mp', 'fsdp'), None)

    def body(x, dy, xn, w1, w2, g1, g2, m1, m2, v1, v2, hp, step):
        nl, b, t, d = x.shape
        T = b * t
        R = w2.shape[1]
        FB = 2 * R
        nc = n // 2
        hbm = pl.BlockSpec(memory_space=pltpu.HBM)
        smem = pl.BlockSpec(memory_space=pltpu.SMEM)
        sd = jax.ShapeDtypeStruct
        state = [sd(w1.shape, F32), sd(w2.shape, F32)] * 3
        res = pl.pallas_call(
            functools.partial(kernel, n),
            out_shape=state + [
                sd((T, d), BF), sd((2 * nl, n, R, d), BF), sd((2 * nl, n, R, d), BF),
                sd((2 * nl, 2, R, d), F32)],
            in_specs=[hbm] * 11 + [smem] * 2,
            out_specs=[hbm] * 10,
            scratch_shapes=[
                pltpu.VMEM((T, d), BF), pltpu.VMEM((d, T), BF),
                pltpu.VMEM((T, d), BF), pltpu.VMEM((d, T), BF),
                pltpu.VMEM((T, FB), BF), pltpu.VMEM((T, FB), BF),
                pltpu.VMEM((max(6 * R, T), d), F32),
                pltpu.VMEM((n, R, d), BF), pltpu.VMEM((n, R, d), BF),
                pltpu.VMEM((2, nc, R, d), BF),
                pltpu.VMEM((2, nc, R, d), F32),
                pltpu.VMEM((2 * nl, R // 2, d), F32), pltpu.VMEM((2 * nl, R // 2, d), F32),
                pltpu.VMEM((2 * nl, R, d), BF),
                pltpu.VMEM((2, n, d // n, FB), BF), pltpu.VMEM((2, 2, R, d), BF),
                pltpu.SemaphoreType.DMA((4 * nl, 10)), pltpu.SemaphoreType.DMA((4 * nl, 10)),
                pltpu.SemaphoreType.DMA((2 * nl, 10)), pltpu.SemaphoreType.DMA((2 * nl, 10)),
                pltpu.SemaphoreType.DMA((2, 2)), pltpu.SemaphoreType.DMA((18,)),
                pltpu.SemaphoreType.DMA((12,)),
            ],
            compiler_params=pltpu.CompilerParams(
                collective_id=0, has_side_effects=True, vmem_limit_bytes=67043328),
        )(x.reshape(nl, T, d), dy.reshape(T, d), xn.reshape(T, d),
          w1, w2, g1, g2, m1, m2, v1, v2, hp, step)
        state = state + [sd((T, d), BF)]
        out = pl.pallas_call(
            copy_out,
            out_shape=state,
            in_specs=[hbm] * 7,
            out_specs=[hbm] * 7,
            scratch_shapes=[pltpu.VMEM(a.shape, a.dtype) for a in state] + [
                pltpu.SemaphoreType.DMA((7, 2)), pltpu.SemaphoreType.DMA((7, 2))],
            compiler_params=pltpu.CompilerParams(vmem_limit_bytes=60 << 20),
        )(*res[:7])
        return tuple(out[:6]) + (out[6].reshape(b, t, d),)

    return jax.shard_map(body, mesh=mesh,
                         in_specs=(tok4, tok3, tok3) + (rows,) * 8 + (P(), P()),
                         out_specs=(rows,) * 6 + (tok3,), check_vma=False)
```

profile of v0, /device:TPU:81, one launch (start us, length us, event | category | flops | bytes accessed | tf_op | source)
XLA Modules:
  0.0 339.9 jit_solution(17226065571911898131)
XLA Ops:
  1.3 326.1 %shard_map.180 = (f32[2,96,3072]{2,1,0:T(8,128)}, f32[2,384,768]{2,1,0:T(8,128)}, f32[2,96,3072]{2,1,0:T(8,128)}, f32[2,384,768]{2,1,0:T(8,128)}, f32[2,96,3072]...) custom-call(bf16[2,2048,768]{2,1,0:T(8,128)(2,1)} %bitcast.4, ...), custom_call_target="tpu_custom_call" | custom-call | tf_op jit(solution)/shard_map/pallas_call | solution.py:668
  327.4 12.4 %shard_map.181 = (f32[2,96,3072]{2,1,0:T(8,128)}, f32[2,384,768]{2,1,0:T(8,128)}, f32[2,96,3072]{2,1,0:T(8,128)}, f32[2,384,768]{2,1,0:T(8,128)}, f32[2,96,3072]...) custom-call(f32[2,96,3072]{2,1,0:T(8,128)} %get-tuple-element.21.refs_0_, ...), custom_call_target="tpu_custom_call" | custom-call | tf_op jit(solution)/shard_map/pallas_call | solution.py:696
where the time goes:
time: 340 us
  Pallas kernels  338 us (99%)
    pallas_call x1, Pallas kernels, body(): pl.pallas_call(functools.partial(kernel, n), out_shape=state + [sd((T, d)...  326 us
    pallas_call x1, Pallas kernels, body(): pl.pallas_call(copy_out, out_shape=state, in_specs=[hbm] * 7, out_specs=[...  12.4 us

commit v1 on v0

--- a/solution.py
+++ b/solution.py
@@ -73,34 +73,29 @@
     for dev in (LEFT, RIGHT, MATE):
         pl.semaphore_signal(barrier, inc=1, device_id={'fsdp': dev})
 
-    pending = {}
-
     def rmake(src, dst, ss, rs, dev):
         return pltpu.make_async_remote_copy(
             src_ref=src[0].at[src[1:]], dst_ref=dst[0].at[dst[1:]], send_sem=ss[0].at[ss[1:]],
             recv_sem=rs[0].at[rs[1:]], device_id={'fsdp': dev})
 
-    def rcopy(key, *a):
-        rmake(*a).start()
-        pending[key] = a
-
     def rwait(dst, ss, rs, dev):
         rmake(dst, dst, ss, rs, dev).wait_recv()
 
-    def sent(key):
-        a = pending.pop(key, None)
-        if a is not None:
-            rmake(*a).wait_send()
+    def rsent(src, ss, rs):
+        rmake(src, src, ss, rs, MATE).wait_send()
 
     class Gather:
-        def __init__(self, ph, m, G, src):
-            self.a, self.m, self.G, self.src = ph * 4 + m, m, G, src
+        def __init__(self, m, G, src):
+            self.m, self.G, self.src = m, G, src
 
         def put(self, t, src, dst, dev):
-            rcopy(('ag', self.a, t), src, dst, (ag_s, self.a, t), (ag_r, self.a, t), dev)
+            rmake(src, dst, (ag_s, self.m), (ag_r, self.m, t), dev).start()
 
         def got(self, t, dst, dev):
-            rwait(dst, (ag_s, self.a, t), (ag_r, self.a, t), dev)
+            rwait(dst, (ag_s, self.m), (ag_r, self.m, t), dev)
+
+        def drain(self):
+            rsent((self.G, self.m, pl.ds(0, n - 1)), (ag_s, self.m), (ag_r, self.m, 0))
 
         def start(self):
             self.start_a()
@@ -150,8 +145,8 @@
             for t in (4, 7, 8, 9):
                 self.mate(t)
 
-    old = [Gather(0, m, go, (nb, m)) for m in range(2 * nl)]
-    new = [Gather(1, m, gn, (nb, m)) for m in range(2 * nl)]
+    old = [Gather(m, go, (nb, m)) for m in range(2 * nl)]
+    new = [Gather(m, gn, (nb, m)) for m in range(2 * nl)]
 
     dest = (co, cr, cl, c)
     mine = tuple(2 * d + k for d in dest)
@@ -163,41 +158,46 @@
     def part(m):
         return p2 if m % 2 else p1
 
-    def rput(m, t, src, dst, dev):
-        rcopy(('rs', m, t), src, dst, (rs_s, m, t), (rs_r, m, t), dev)
-
-    def rgot(m, t, dst, dev):
-        rwait(dst, (rs_s, m, t), (rs_r, m, t), dev)
-
-    def x0_copy(m, sl):
-        return rmake((part(m), theirs[sl]), (pq, rset(m), sl), (rs_s, m, sl), (rs_r, m, sl), MATE)
+    def rput(m, p, e, src, dst, dev):
+        rmake(src, dst, (rs_s, m, p), (rs_r, m, e), dev).start()
+
+    def rgot(m, e, dst, dev):
+        rwait(dst, (rs_s, m, 0), (rs_r, m, e), dev)
 
     def rs_x0(m, sl):
-        x0_copy(m, sl).start()
+        rput(m, 0, sl, (part(m), theirs[sl]), (pq, rset(m), sl), MATE)
+
+    def rs_x0_done(m):
+        rsent((pq, rset(m)), (rs_s, m, 0), (rs_r, m, 0))
+
+    def rs_pair_done(m):
+        rsent((rp, m), (rs_s, m, 1), (rs_r, m, 6))
+
+    def rs_mid_done(m):
+        rsent((rp, m, 0), (rs_s, m, 2), (rs_r, m, 6))
 
     def rs_pair(m, sl):
         s = rset(m)
-        for t in {0: (4, 5), 1: (6,), 2: (7,), 3: ()}[sl]:
-            sent(('rs', m + 2, t))
+        if sl == 0 and m + 2 < 2 * nl:
+            rs_pair_done(m + 2)
         rgot(m, sl, (pq, s, sl), MATE)
-        x0_copy(m, sl).wait_send()
         tb[s, sl] = part(m)[mine[sl]].astype(F32) + pq[s, sl].astype(F32)
         if sl == 0:
-            rput(m, 4, (tb, s, 0, hA), (ra, m), LEFT)
-            rput(m, 5, (tb, s, 0, hB), (rb, m), RIGHT)
+            rput(m, 1, 4, (tb, s, 0, hA), (ra, m), LEFT)
+            rput(m, 1, 5, (tb, s, 0, hB), (rb, m), RIGHT)
         elif sl == 1:
-            rput(m, 6, (tb, s, 1, hA), (rp, m, 0, hA), RIGHT)
+            rput(m, 1, 6, (tb, s, 1, hA), (rp, m, 0, hA), RIGHT)
         elif sl == 2:
-            rput(m, 7, (tb, s, 2, hB), (rp, m, 1, hB), LEFT)
+            rput(m, 1, 6, (tb, s, 2, hB), (rp, m, 1, hB), LEFT)
 
     def rs_mid(m):
         s = rset(m)
         rgot(m, 4, (ra, m), RIGHT)
         ra[m] = ra[m] + tb[s, 2, hA]
-        rput(m, 8, (ra, m), (rp, m, 1, hA), LEFT)
+        rput(m, 2, 6, (ra, m), (rp, m, 1, hA), LEFT)
         rgot(m, 5, (rb, m), LEFT)
         rb[m] = rb[m] + tb[s, 1, hB]
-        rput(m, 9, (rb, m), (rp, m, 0, hB), RIGHT)
+        rput(m, 2, 6, (rb, m), (rp, m, 0, hB), RIGHT)
 
     def pieces(m, arr, row):
         l = m // 2
@@ -212,33 +212,25 @@
         cps = []
         for j, arr in enumerate(ins[m % 2]):
             for hbm, vm in pieces(m, arr, j * R):
-                cps.append(pltpu.make_async_copy(hbm, vm, lsem.at[len(cps)]))
+                cps.append(pltpu.make_async_copy(hbm, vm, lsem.at[j]))
         return cps
 
     def adam_load(m):
         for cp in adam_copies(m):
             cp.start()
 
-    def adam_outs(m):
-        cps = []
-        for arr, row in zip(outs[m % 2], (0, 2 * R, 3 * R)):
-            for hbm, vm in pieces(m, arr, row):
-                cps.append(pltpu.make_async_copy(vm, hbm, osem.at[len(cps)]))
-        return cps
+    def arrived(row, rows, sem):
+        pltpu.make_async_copy(acc.at[pl.ds(row, rows)], acc.at[pl.ds(row, rows)], sem).wait()
 
     def adam_run(m):
         s = rset(m)
-        for t, dst, dev in ((6, (rp, m, 0, hA), LEFT), (9, (rp, m, 0, hB), LEFT),
-                            (8, (rp, m, 1, hA), RIGHT), (7, (rp, m, 1, hB), RIGHT)):
-            rgot(m, t, dst, dev)
-        cps = [pltpu.make_async_copy(rp.at[m, e], acc.at[pl.ds((4 + e) * R, R)], lsem.at[16 + e])
-               for e in range(2)]
-        for cp in cps:
-            cp.start()
-        for cp in adam_copies(m) + cps:
-            cp.wait()
-        for t in range(5):
-            sent(('ag', m, t))
+        rgot(m, 6, (rp, m), LEFT)
+        for e in range(2):
+            pltpu.make_async_copy(rp.at[m, e], acc.at[pl.ds((4 + e) * R, R)], lsem.at[4]).start()
+        for j in range(4):
+            arrived(j * R, R, lsem.at[j])
+        arrived(4 * R, 2 * R, lsem.at[4])
+        old[m].drain()
         lr, b1, b2, eps, wd = [hp[j] for j in range(5)]
         c1 = 1.0 - ipow(b1, step[0])
         c2 = 1.0 - ipow(b2, step[0])
@@ -260,12 +252,13 @@
             acc[rows[3]] = vn
             nb[m, pl.ds(o, ch)] = wn.astype(BF)
 
-        for cp in adam_outs(m):
-            cp.start()
+        for e, (arr, j) in enumerate(zip(outs[m % 2], (0, 2, 3))):
+            for hbm, vm in pieces(m, arr, j * R):
+                pltpu.make_async_copy(vm, hbm, osem.at[e]).start()
 
     def adam_done(m):
-        for cp in adam_outs(m):
-            cp.wait()
+        for e, j in enumerate((0, 2, 3)):
+            arrived(j * R, R, osem.at[e])
 
     def wcopy(G, l, q, slot, kind):
         if kind:
@@ -413,8 +406,8 @@
     scope = jax.named_scope
 
     with scope('start'):
-        w_in = [[pltpu.make_async_copy(a, b, lsem.at[m * 4 + e])
-                 for e, (a, b) in enumerate(pieces(m, ins[m % 2][0], m * R))] for m in range(2 * nl)]
+        w_in = [[pltpu.make_async_copy(a, b, lsem.at[m]) for a, b in pieces(m, ins[m % 2][0], m * R)]
+                for m in range(2 * nl)]
         for m in (2, 3, 0, 1):
             for cp in w_in[m]:
                 cp.start()
@@ -424,8 +417,7 @@
             cp.start()
         own_out = [pltpu.make_async_copy(nb.at[m], go.at[m, i], osem.at[m]) for m in range(2 * nl)]
         for m in (2, 3, 0, 1):
-            for cp in w_in[m]:
-                cp.wait()
+            arrived(m * R, R, lsem.at[m])
             nb[m] = acc[pl.ds(m * R, R), :].astype(BF)
             if m == 2:
                 pl.semaphore_wait(barrier, 3)
@@ -474,10 +466,12 @@
         ('D2', lambda j, q, s: bwd_dx(s, j == 0), {}),
     ])
     with scope('mid2'):
-        xin = pltpu.make_async_copy(x.at[0], xb, lsem.at[0])
+        xin = pltpu.make_async_copy(x.at[0], xb, lsem.at[5])
         xin.start()
+        rs_x0_done(3)
         for sl in range(4):
             rs_pair(2, sl)
+        rs_x0_done(2)
     with scope('tr2'):
         narrow(yb)
         transpose(yt, yb)
@@ -585,49 +579,55 @@
         r = pl.ds(t * TF if isinstance(t, int) else pl.multiple_of(t * TF, TF), TF)
         return pltpu.make_async_copy(xb.at[r], zo.at[r], lsem.at[t])
 
-    with scope('F2a'):
+    def right_in():
+        new[3].mate(8)
+        new[3].mate(7)
+        w2c[1].start()
+        w2c[2].start()
+
+    def opposite_in():
+        new[3].mate(9)
+        w2c[3].start()
+
+    with scope('F2H0'):
         new[3].mate(4)
         w1c[0].start()
         w2c[0].start()
         w1c[1].start()
         w1c[0].wait()
         step(hj=0)
-    with scope('F2b'):
-        new[3].fwd_a()
+    with scope('F2P0'):
+        w2c[0].wait()
         w1c[2].start()
+        step(pj=0, hook=new[3].fwd_a)
+    with scope('F2H1'):
         w1c[1].wait()
-        w2c[0].wait()
-        step(hj=1, pj=0)
-    def right_in():
-        new[3].mate(8)
-        new[3].mate(7)
-        w2c[1].start()
-        w2c[2].start()
-
-    def opposite_in():
-        new[3].mate(9)
-        w2c[3].start()
-
-    with scope('F2c'):
-        new[3].fwd_b()
+        step(hj=1)
+    with scope('F2H2'):
         w1c[3].start()
         w1c[2].wait()
-        step(hj=2, hook=right_in)
-    with scope('F2d'):
+        step(hj=2, hook=new[3].fwd_b)
+    with scope('F2H3'):
         w1c[3].wait()
+        step(hj=3, hook=right_in)
+    with scope('F2P1'):
         w2c[1].wait()
-        step(hj=3, pj=1, hook=new[3].fin)
-    with scope('F2e'):
+        step(pj=1, hook=new[3].fin)
+    with scope('F2P2'):
         w2c[2].wait()
         step(pj=2, hook=opposite_in)
-    with scope('F2f'):
+    with scope('F2P3'):
         w2c[3].wait()
         step(pj=3, last=True)
     with scope('end'):
         for t in range(T // TF):
             zout(t).wait()
-        for key in list(pending):
-            sent(key)
+        for m in range(2 * nl):
+            new[m].drain()
+            rs_mid_done(m)
+        for m in range(2):
+            rs_x0_done(m)
+            rs_pair_done(m)
 
 
 def copy_out(*refs):
@@ -683,10 +683,10 @@
                 pltpu.VMEM((2 * nl, R // 2, d), F32), pltpu.VMEM((2 * nl, R // 2, d), F32),
                 pltpu.VMEM((2 * nl, R, d), BF),
                 pltpu.VMEM((2, n, d // n, FB), BF), pltpu.VMEM((2, 2, R, d), BF),
-                pltpu.SemaphoreType.DMA((4 * nl, 10)), pltpu.SemaphoreType.DMA((4 * nl, 10)),
-                pltpu.SemaphoreType.DMA((2 * nl, 10)), pltpu.SemaphoreType.DMA((2 * nl, 10)),
-                pltpu.SemaphoreType.DMA((2, 2)), pltpu.SemaphoreType.DMA((18,)),
-                pltpu.SemaphoreType.DMA((12,)),
+                pltpu.SemaphoreType.DMA((2 * nl,)), pltpu.SemaphoreType.DMA((2 * nl, 10)),
+                pltpu.SemaphoreType.DMA((2 * nl, 3)), pltpu.SemaphoreType.DMA((2 * nl, 7)),
+                pltpu.SemaphoreType.DMA((2, 2)), pltpu.SemaphoreType.DMA((6,)),
+                pltpu.SemaphoreType.DMA((4,)),
             ],
             compiler_params=pltpu.CompilerParams(
                 collective_id=0, has_side_effects=True, vmem_limit_bytes=67043328),

time: 340 us -> 337 us (level)
  no operation moved by 1% of the time
where the time goes in v1:
time: 337 us
  Pallas kernels  336 us (100%)
    pallas_call x1, Pallas kernels, body(): pl.pallas_call(functools.partial(kernel, n), out_shape=state + [sd((T, d)...  323 us
    pallas_call x1, Pallas kernels, body(): pl.pallas_call(copy_out, out_shape=state, in_specs=[hbm] * 7, out_specs=[...  12.4 us

profile of v1, /device:TPU:81, one launch (start us, length us, event | category | flops | bytes accessed | tf_op | source)
XLA Modules:
  0.0 337.1 jit_solution(11453996337775005485)
XLA Ops:
  1.3 323.3 %shard_map.180 = (f32[2,96,3072]{2,1,0:T(8,128)}, f32[2,384,768]{2,1,0:T(8,128)}, f32[2,96,3072]{2,1,0:T(8,128)}, f32[2,384,768]{2,1,0:T(8,128)}, f32[2,96,3072]...) custom-call(bf16[2,2048,768]{2,1,0:T(8,128)(2,1)} %bitcast.4, ...), custom_call_target="tpu_custom_call" | custom-call | tf_op jit(solution)/shard_map/pallas_call | solution.py:668
  324.6 12.4 %shard_map.181 = (f32[2,96,3072]{2,1,0:T(8,128)}, f32[2,384,768]{2,1,0:T(8,128)}, f32[2,96,3072]{2,1,0:T(8,128)}, f32[2,384,768]{2,1,0:T(8,128)}, f32[2,96,3072]...) custom-call(f32[2,96,3072]{2,1,0:T(8,128)} %get-tuple-element.21.refs_0_, ...), custom_call_target="tpu_custom_call" | custom-call | tf_op jit(solution)/shard_map/pallas_call | solution.py:696
